TPU v7x, 32 devices: a whole 2x2x4 slice. The times are simulated.
32 devices in a mesh: batch: 4 (over z), seq: 8 (over y, x, core).
Axes of the slice: x: 2, y: 2, z: 4, core: 2. Of those that a mesh axis runs over, the one named last changes fastest.
Arguments:
- tokens: bfloat16 [2, 64, 8192], P(None, 'batch', 'seq'), may hold values from -8 to 8
- norm_gain: bfloat16 [8192], P('seq'), may hold values from 0.5 to 1.5
- w_qkv: bfloat16 [8192, 10240], P('batch', 'seq'), may hold values from -0.0625 to 0.0625
- w_out: bfloat16 [8192, 8192], P('seq'), may hold values from -0.75 to 0.75
- cache_keys: bfloat16 [64, 1024, 1024], P('batch', 'seq'), may hold values from -120 to 120
- cache_values: bfloat16 [64, 1024, 1024], P('batch', 'seq'), may hold values from -6 to 6
- lengths: int32 [64], P('batch'), may hold values from 256 to 1022
- positions: int32 [64], P('batch'), may hold values from 0 to 4095
Outputs:
- mixed: bfloat16 [2, 64, 8192], P(None, 'batch', 'seq')
Inputs may be any that keep to these rules, and one draw needn't show every extreme that they name: `lengths`: filled cache positions of a sequence; its two new tokens take the next two positions.
All inputs are finite; a program needn't handle non-finite values.
Results may differ from a plain program's by a relative error of at most 0.01255.
The roundings to bfloat16 on the way count: a program that leaves them out, or rounds other values in their place, can miss the bound.
Values may be sent and summed in bfloat16 or wider, within the bound.
A program may use at most 128 MiB of HBM per device.

v0:
```python
import math

import jax
import jax.numpy as jnp
from jax import lax
from jax.sharding import PartitionSpec as P

D = 8192
H = 64
KVH = 8
HD = 128


rope_base = 500000.0
epsilon = 1e-05
lowest = -1e30


def rotate(heads, places):
    half = heads.shape[-1] // 2
    freqs = rope_base ** (-(jnp.arange(half).astype(jnp.float32) * 2.0) / heads.shape[-1])
    angles = places[:, None, None] * freqs
    cosine = jnp.cos(angles)
    sine = jnp.sin(angles)
    first = heads[..., :half]
    second = heads[..., half:]
    return jnp.concatenate([first * cosine - second * sine, second * cosine + first * sine], -1)


def shards(tokens, norm_gain, w_qkv, w_out, cache_keys, cache_values, lengths, positions):
    seqs = tokens.shape[1]
    local_width = tokens.shape[2]
    rows = 2 * seqs
    group = H // KVH
    query_width = H * HD
    pair_width = KVH * HD
    scale = 1.0 / math.sqrt(HD)
    flat = tokens.reshape(rows, local_width)
    widened = flat.astype(jnp.float32)
    totals = lax.psum(jnp.sum(widened * widened, -1), "seq")
    local = (
        widened * lax.rsqrt(totals[:, None] / D + epsilon) * norm_gain.astype(jnp.float32)
    ).astype(jnp.bfloat16)
    normed = lax.all_gather(local, "seq", axis=1, tiled=True)
    moved = lax.all_to_all(normed, "batch", split_axis=1, concat_axis=0, tiled=True)
    projected = lax.psum_scatter(
        jnp.dot(moved, w_qkv, preferred_element_type=jnp.float32),
        "batch",
        scatter_dimension=0,
        tiled=True,
    ).astype(jnp.bfloat16)
    projected = lax.all_gather(projected, "seq", axis=1, tiled=True)
    places = jnp.concatenate([positions, positions + 1]).astype(jnp.float32)
    queries = rotate(
        projected[:, :query_width].astype(jnp.float32).reshape(rows, H, HD), places
    ).astype(jnp.bfloat16)
    fresh_keys = rotate(
        projected[:, query_width : query_width + pair_width]
        .astype(jnp.float32)
        .reshape(rows, KVH, HD),
        places,
    ).astype(jnp.bfloat16)
    fresh_values = projected[:, query_width + pair_width :].reshape(2, seqs, KVH, HD)
    queries = queries.reshape(2, seqs, KVH, group, HD)
    fresh_keys = fresh_keys.reshape(2, seqs, KVH, HD)
    index = lax.axis_index("seq")
    shard_len = cache_keys.shape[1]
    keys_local = cache_keys.reshape(seqs, shard_len, KVH, HD)
    values_local = cache_values.reshape(seqs, shard_len, KVH, HD)
    scores = (
        jnp.einsum("tbkgd,bnkd->tbkgn", queries, keys_local, preferred_element_type=jnp.float32)
        * scale
    )
    extra_scores = (
        jnp.einsum("tbkgd,jbkd->tbkgj", queries, fresh_keys, preferred_element_type=jnp.float32)
        * scale
    )
    global_rows = index * shard_len + jnp.arange(shard_len)
    live_cache = (global_rows[None, :] < lengths[:, None])[None, :, None, None, :]
    steps_index = jnp.arange(2)
    owner = (lengths[:, None] + steps_index[None, :]) // shard_len == index
    causal = steps_index[None, :] <= steps_index[:, None]
    live_extra = (owner[None, :, :] & causal[:, None, :])[:, :, None, None, :]
    local_peak = jnp.maximum(
        jnp.max(jnp.where(live_cache, scores, lowest), -1),
        jnp.max(jnp.where(live_extra, extra_scores, lowest), -1),
    )
    weights = jnp.where(live_cache, jnp.exp(scores - local_peak[..., None]), 0.0)
    extra_weights = jnp.where(live_extra, jnp.exp(extra_scores - local_peak[..., None]), 0.0)
    total = jnp.sum(weights, -1) + jnp.sum(extra_weights, -1)
    summed = jnp.einsum(
        "tbkgn,bnkd->tbkgd",
        weights.astype(jnp.bfloat16),
        values_local,
        preferred_element_type=jnp.float32,
    )
    summed = summed + jnp.einsum(
        "tbkgj,jbkd->tbkgd",
        extra_weights.astype(jnp.bfloat16),
        fresh_values,
        preferred_element_type=jnp.float32,
    )
    summed = summed.reshape(rows, H, HD)
    total = total.reshape(rows, H)
    local_peak = local_peak.reshape(rows, H)
    peak = lax.pmax(local_peak, "seq")
    factor = jnp.exp(local_peak - peak)
    summed = summed * factor[..., None]
    total = total * factor
    summed_all, total_all = lax.psum((summed, total), "seq")
    heads_here = H // lax.axis_size("seq")
    mine = lax.dynamic_slice_in_dim(summed_all, index * heads_here, heads_here, 1)
    mine_total = lax.dynamic_slice_in_dim(total_all, index * heads_here, heads_here, 1)
    attended = (mine / mine_total[..., None]).astype(jnp.bfloat16).reshape(rows, -1)
    partial_value = jnp.dot(attended, w_out, preferred_element_type=jnp.float32)
    columns = lax.psum_scatter(partial_value, "seq", scatter_dimension=1, tiled=True)
    return (flat.astype(jnp.float32) + columns).astype(jnp.bfloat16).reshape(2, seqs, local_width)


def solution(mesh):
    return jax.shard_map(
        shards,
        mesh=mesh,
        in_specs=(
            P(None, "batch", "seq"),
            P("seq"),
            P("batch", "seq"),
            P("seq", None),
            P("batch", "seq", None),
            P("batch", "seq", None),
            P("batch"),
            P("batch"),
        ),
        out_specs=P(None, "batch", "seq"),
        check_vma=False,
    )
```

profile of v0, /device:TPU:0, one launch (start us, length us, event | category | flops | bytes accessed | tf_op | source)
XLA Modules:
  0.0 237.8 jit_solution(1778897422490928366)
XLA Ops:
  6.5 0.9 fusion.25
  7.6 15.1 %psum.21 = f32[32]{0:T(128)S(1)} all-reduce(f32[32]{0:T(128)S(1)} %reduce_sum.30), channel_id=1, replica_groups=mesh['batch'=4,'seq'=8] {'seq'}, use_global_device_ids=true, to_apply=%region_1.0 | all-reduce | flops 32 | bytes 256 | tf_op jit(solution)/shard_map/psum | solution.py:40
  24.3 8.8 %all_gather.6 = bf16[32,8192]{1,0:T(8,128)(2,1)S(1)} all-gather(bf16[32,1024]{1,0:T(8,128)(2,1)S(1)} %fusion.27), channel_id=1, replica_groups=mesh['batch'=4,'seq'=8] {'seq'}, dimensions={1}, use_global_device_ids=true | all-gather | bytes 589824 | tf_op jit(solution)/shard_map/all_gather | solution.py:44
  34.0 4.9 %all-to-all-start = ((bf16[32,4,2048]{2,0,1:T(8,128)(2,1)}), bf16[32,4,2048]{2,0,1:T(8,128)(2,1)S(1)}, u32[]{:S(2)}, u32[]{:S(2)}) async-start(bf16[32,4,2048]{2,0,1:T(8,128)(2,1)} %bitcast.76), calls=%async_computation | async-start | bytes 1048576 | tf_op jit(solution)/shard_map/all_to_all | solution.py:45
  38.9 5.4 %copy.51 = bf16[256,8,8,128]{3,2,1,0:T(8,128)(2,1)} copy(bf16[256,8,8,128]{3,1,2,0:T(8,128)(2,1)} %bitcast.83) | data formatting | bytes 8388608
  44.3 3.1 %copy.53 = bf16[256,8,8,128]{3,2,1,0:T(8,128)(2,1)} copy(bf16[256,8,8,128]{3,1,2,0:T(8,128)(2,1)S(1)} %bitcast.84) | data formatting | bytes 8388608
  47.6 6.3 %all-to-all-done = bf16[32,4,2048]{2,0,1:T(8,128)(2,1)S(1)} async-done(((bf16[32,4,2048]{2,0,1:T(8,128)(2,1)}), bf16[32,4,2048]{2,0,1:T(8,128)(2,1)S(1)}, u32[]{:S(2)}, u32[]{:S(2)}) %all-to-all-start) | async-done | bytes 524320 | tf_op jit(solution)/shard_map/all_to_all | solution.py:45
  53.9 4.2 %fusion.45 = f32[128,1280]{1,0:T(8,128)} fusion(bf16[128,2048]{1,0:T(8,128)(2,1)S(1)} %bitcast.90, bf16[2048,1280]{1,0:T(8,128)(2,1)} %param.10), kind=kOutput, calls=%fused_computation.78 | convolution fusion | flops 671088640 | bytes 6422528 | tf_op jit(solution)/shard_map/dot_general | solution.py:47
  58.4 4.7 %bitcast_bitcast_fusion.1 = bf16[16,128,8,128,1]{3,2,1,0,4:T(8,128)(2,1)} fusion(bf16[16,128,8,128]{3,2,1,0:T(8,128)(2,1)} %bitcast.81), kind=kLoop, calls=%fused_computation.1 | loop fusion | bytes 8388608 | tf_op jit(solution)/shard_map/reshape | solution.py:68
  63.1 2.2 bitcast_bitcast_fusion
  65.3 13.7 %reduce-scatter.3.cloned.1.call-done = f32[32,1280]{1,0:T(8,128)} async-done(((f32[128,1280]{1,0:T(8,128)}), f32[32,1280]{1,0:T(8,128)}) %reduce-scatter.3.cloned.1.call-update) | async-done | bytes 163856 | tf_op jit(solution)/shard_map/reduce_scatter | solution.py:46
  80.0 10.4 %all_gather.7 = bf16[32,10240]{1,0:T(8,128)(2,1)S(1)} all-gather(bf16[32,1280]{1,0:T(8,128)(2,1)S(1)} %convert_element_type.57), channel_id=1, replica_groups=mesh['batch'=4,'seq'=8] {'seq'}, dimensions={1}, use_global_device_ids=true | all-gather | bytes 737280 | tf_op jit(solution)/shard_map/all_gather | solution.py:52
  91.5 1.0 copy-done
  92.5 2.5 %select_reduce_fusion = (f32[2,16,8,8]{3,0,2,1:T(2,128)S(1)}, f32[2,16,8,8,128]{4,3,0,2,1:T(8,128)S(1)}) fusion(pred[16,128]{1,0:T(8,128)(4,1)S(1)} %broadcast_compare_fusion, bf16[16,128,8,128,1]{3,2,1,0,4:T(8,128)(2,1)S(1)} %copy-done, bf16[2,16,8,8,64]{4,3,2,1,0:T(8,128)(2,1)S(1)} %bitcast.88, bf16[2,16,8,8,64]{4,3,2,1,0:T(8,128)(2,1)S(1)} %bitcast.86), kind=kOutput, calls=%fused_computation.15 | convolution fusion | flops 68941824 | bytes 5777408 | tf_op jit(solution)/shard_map/tbkgd,bnkd->tbkgn/dot_general | solution.py:71
  95.0 2.6 %select_reduce_fusion.1 = (f32[2,16,8,8]{3,0,2,1:T(2,128)S(1)}, f32[2,16,8,8,2]{3,4,0,2,1:T(2,128)S(1)}) fusion(pred[2,16,2]{2,0,1:T(4,128)(4,1)S(1)} %broadcast_and_fusion, bf16[2,16,8,64]{3,0,2,1:T(2,128)(2,1)S(1)} %copy.30, bf16[2,16,8,64]{3,0,2,1:T(2,128)(2,1)S(1)} %copy.29, bf16[2,16,8,8,64]{4,3,2,1,0:T(8,128)(2,1)S(1)} %bitcast.89, ...), kind=kOutput, calls=%fused_computation.29 | convolution fusion | flops 2238464 | bytes 614464 | tf_op jit(solution)/shard_map/tbkgd,jbkd->tbkgj/dot_general | solution.py:75
  98.0 23.6 %pmax.7 = f32[32,64]{0,1:T(8,128)S(1)} all-reduce(f32[32,64]{0,1:T(8,128)S(1)} %max.14), channel_id=1, replica_groups=mesh['batch'=4,'seq'=8] {'seq'}, use_global_device_ids=true, to_apply=%region_5.6 | all-reduce | flops 2048 | bytes 16384 | tf_op jit(solution)/shard_map/pmax | solution.py:106
  123.8 3.4 %fusion.13 = f32[2,16,8,8,128]{4,3,0,2,1:T(8,128)S(1)} fusion(f32[2,16,8,8,128]{4,3,0,2,1:T(8,128)S(1)} %convolution_bitcast_fusion, bf16[16,128,8,128,1]{3,2,1,0,4:T(8,128)(2,1)} %bitcast_bitcast_fusion, f32[2,16,8,8,128]{4,3,0,2,1:T(8,128)S(1)} %get-tuple-element.16, f32[2,16,8,8]{3,0,2,1:T(2,128)S(1)} %max.13, pred[16,128]{1,0:T(8,128)(4,1)S(1)} %broadcast_compare_fusion), kind=kOutput, calls=%fused_computation.9 | convolution fusion | flops 68157440 | bytes 7350272 | tf_op jit(solution)/shard_map/tbkgn,bnkd->tbkgd/dot_general | solution.py:91
  127.4 1.4 broadcast_multiply_fusion
  128.9 22.6 %psum.23 = f32[32,64]{0,1:T(8,128)S(1)} all-reduce(f32[32,64]{0,1:T(8,128)S(1)} %get-tuple-element.5), channel_id=1, replica_groups=mesh['batch'=4,'seq'=8] {'seq'}, use_global_device_ids=true, to_apply=%region_9.10 | all-reduce | flops 2048 | bytes 16384 | tf_op jit(solution)/shard_map/psum | solution.py:110
  151.5 32.0 %all-reduce.2.cloned.1.call-done = f32[32,64,128]{2,1,0:T(8,128)} async-done(((f32[32,64,128]{2,1,0:T(8,128)}), f32[32,64,128]{2,1,0:T(8,128)}) %all-reduce.2.cloned.1.call-update) | async-done | bytes 1048592 | tf_op jit(solution)/shard_map/psum | solution.py:110
  183.5 1.0 divide_convert_fusion
  184.5 9.8 %fusion.30 = f32[32,8192]{1,0:T(8,128)} fusion(bf16[1024,8192]{1,0:T(8,128)(2,1)} %param.11, bf16[4,8,8,128]{3,2,1,0:T(8,128)(2,1)S(1)} %bitcast.93), kind=kOutput, calls=%fused_computation.42 | convolution fusion | flops 536870912 | bytes 17891328 | tf_op jit(solution)/shard_map/dot_general | solution.py:115
  194.3 35.4 %reduce-scatter.5.cloned.1.call-done = f32[32,1024]{1,0:T(8,128)} async-done(((f32[32,8192]{1,0:T(8,128)}), f32[32,1024]{1,0:T(8,128)}) %reduce-scatter.5.cloned.1.call-update) | async-done | bytes 131088 | tf_op jit(solution)/shard_map/reduce_scatter | solution.py:116
  229.7 1.5 fusion.28
  (56 shorter events, 7.9 us)
Async XLA Ops:
  34.0 19.9 %all-to-all-start = ((bf16[32,4,2048]{2,0,1:T(8,128)(2,1)}), bf16[32,4,2048]{2,0,1:T(8,128)(2,1)S(1)}, u32[]{:S(2)}, u32[]{:S(2)}) async-start(bf16[32,4,2048]{2,0,1:T(8,128)(2,1)} %bitcast.76), calls=%async_computation | async-start | bytes 1048576 | tf_op jit(solution)/shard_map/all_to_all | solution.py:45
  38.9 40.2 %reduce-scatter.3.cloned.1.call-start = ((), (), s32[]{:S(2)}) async-start(), calls=%async_computation.3 | async-start | bytes 819200 | tf_op jit(solution)/shard_map/reduce_scatter | solution.py:46
  38.9 5.4 %copy-start.2 = (bf16[16,128,1024]{2,1,0:T(8,128)(2,1)S(1)}, bf16[16,128,1024]{2,1,0:T(8,128)(2,1)}, u32[]{:S(2)}) copy-start(bf16[16,128,1024]{2,1,0:T(8,128)(2,1)} %param.13) | copy-start | bytes 12582916
  44.3 3.1 %copy-start.5 = (s32[16]{0:T(128)S(1)}, s32[16]{0:T(128)}, u32[]{:S(2)}) copy-start(s32[16]{0:T(128)} %param.15) | copy-start | bytes 196
  44.3 3.2 %copy-start.4 = (s32[16]{0:T(128)S(1)}, s32[16]{0:T(128)}, u32[]{:S(2)}) copy-start(s32[16]{0:T(128)} %param.14) | copy-start | bytes 196
  58.1 125.3 %all-reduce.2.cloned.1.call-start = ((), (), s32[]{:S(2)}) async-start(), calls=%async_computation.4 | async-start | bytes 2097152 | tf_op jit(solution)/shard_map/psum | solution.py:110
  58.4 4.7 %copy-start.1 = (bf16[256,8,8,128]{3,2,1,0:T(8,128)(2,1)S(1)}, bf16[256,8,8,128]{3,2,1,0:T(8,128)(2,1)}, u32[]{:S(2)}) copy-start(bf16[256,8,8,128]{3,2,1,0:T(8,128)(2,1)} %copy.53) | copy-start | bytes 12582916
  90.3 2.2 copy-start
  128.8 100.9 %reduce-scatter.5.cloned.1.call-start = ((), (), s32[]{:S(2)}) async-start(), calls=%async_computation.5 | async-start | bytes 1179648 | tf_op jit(solution)/shard_map/reduce_scatter | solution.py:116
  184.5 45.2 %copy-start.3 = (bf16[2,16,1024]{2,1,0:T(8,128)(2,1)S(1)}, bf16[2,16,1024]{2,1,0:T(8,128)(2,1)}, u32[]{:S(2)}) copy-start(bf16[2,16,1024]{2,1,0:T(8,128)(2,1)} %param.8) | copy-start | bytes 196612
Sparse Core Ops, SparseCore 0:
  58.2 20.7 reduce-scatter.2
  128.9 54.4 all-reduce.1
  194.4 35.2 reduce-scatter.4
where the time goes:
time: 238 us
  waiting for transfers between devices  87.4 us (37%)
  blocking collectives  80.6 us (34%)
  matrix products  23.1 us (10%)
  local copies, waits for them, and re-layouts  18.4 us (8%)
  between operations  13.3 us (6%)
  other arithmetic  10 us (4%)
  starting transfers between devices  4.96 us (2%)
    reduce_scatter x1, waiting for transfers between devices, shards(): lax.psum_scatter(partial_value, 'seq', scatter_dimension=1, tiled=True)  35.4 us
    psum x1, waiting for transfers between devices, shards(): summed_all, total_all = lax.psum((summed, total), 'seq')  32 us
    pmax x1, blocking collectives, shards(): peak = lax.pmax(local_peak, 'seq')  23.6 us
    psum x1, blocking collectives, shards(): summed_all, total_all = lax.psum((summed, total), 'seq')  22.6 us
    psum x1, blocking collectives, shards(): totals = lax.psum(jnp.sum(widened * widened, -1), 'seq')  15.1 us
    reduce_scatter x1, waiting for transfers between devices, shards(): lax.psum_scatter(jnp.dot(moved, w_qkv, preferred_element_type=jnp.float32...  13.7 us
    all_gather x1, blocking collectives, shards(): projected = lax.all_gather(projected, 'seq', axis=1, tiled=True)  10.4 us
    dot_general x1, matrix products, shards(): partial_value = jnp.dot(attended, w_out, preferred_element_type=jnp.float32)  9.78 us
  transfers between devices with their start and end apart: 4, of which 4 were waited for; matrix products, arithmetic and copies ran while one was open for 7% of the time, Pallas kernels for 0%

commit v1 on v0

v1 whole, which is shorter than its diff:
```python
import math

import jax
import jax.numpy as jnp
from jax import lax
from jax.experimental import pallas as pl
from jax.experimental.pallas import tpu as pltpu
from jax.sharding import PartitionSpec as P

D = 8192
H = 64
KVH = 8
HD = 128
LANES = 128
PAD = 16
MESH = pl.DeviceIdType.MESH

rope_base = 500000.0
epsilon = 1e-05
lowest = -1e30


def flip(index, bits):
    result = index
    step = 1
    while step <= bits:
        if bits & step:
            result = result + step * (1 - 2 * ((index // step) % 2))
        step *= 2
    return result


def remote(src, dst, send_sem, recv_sem, batch, seq):
    return pltpu.make_async_remote_copy(
        src_ref=src,
        dst_ref=dst,
        send_sem=send_sem,
        recv_sem=recv_sem,
        device_id=(batch, seq),
        device_id_type=MESH,
    )


def signal(sem, batch, seq):
    pl.semaphore_signal(sem, inc=1, device_id=(batch, seq), device_id_type=MESH)


def project_kernel(
    nbatch, nseq, x_ref, gain_ref, w_hbm, out_ref,
    wbuf, stat_send, stat_recv, normed, slots, part, part_recv, gath,
    w_sem, s1, r1, s2, r2, s3, r3, s4, r4,
):
    b = lax.axis_index("batch")
    s = lax.axis_index("seq")
    sub = nseq // nbatch
    rows, local = x_ref.shape
    width = wbuf.shape[1]
    w_copy = pltpu.make_async_copy(w_hbm, wbuf, w_sem)
    w_copy.start()

    home = s // sub
    place = s % sub
    at_home = home == b
    barrier = pltpu.get_barrier_semaphore()
    for k in range(1, nseq):
        signal(barrier, b, flip(s, k))
    for k in range(1, nbatch):
        signal(barrier, flip(b, k), s)
    for source in range(nbatch):
        for j in range(sub):
            @pl.when(jnp.logical_not((source == b) & (b * sub + j == s)))
            def _():
                signal(barrier, source, b * sub + j)

    widened = x_ref[...].astype(jnp.float32)
    sums = jnp.sum(widened * widened, -1, keepdims=True)
    tiles = rows // 8
    span = LANES // tiles
    lane = lax.broadcasted_iota(jnp.int32, (8, LANES), 1) // span
    packed = jnp.zeros((8, LANES), jnp.float32)
    for i in range(tiles):
        packed = jnp.where(lane == i, sums[i * 8 : (i + 1) * 8], packed)
    stat_send[...] = packed

    pl.semaphore_wait(barrier, (nseq - 1) + (nbatch - 1) + nseq - jnp.where(at_home, 1, 0))

    copies = []
    for k in range(nseq - 1, 0, -1):
        copies.append(remote(stat_send, stat_recv.at[k], s1.at[k], r1.at[k], b, flip(s, k)))
        copies[-1].start()
    total = packed
    for copy in copies:
        copy.wait_recv()
    for k in range(1, nseq):
        total = total + stat_recv[k]
    gain = gain_ref[...].astype(jnp.float32)
    inverse = lax.rsqrt(total / D + epsilon)
    column = jnp.concatenate([inverse[:, i * span : i * span + 1] for i in range(tiles)], 0)
    normed[...] = (widened * column * gain).astype(jnp.bfloat16)

    mine = pl.ds(pl.multiple_of(b * rows, rows), rows)
    sends = []
    for k in range(nseq - 1, 0, -1):
        sends.append(
            remote(normed, slots.at[place, mine], s2.at[k], r2.at[b, place], home, flip(s, k))
        )
        sends[-1].start()
    straight = remote(normed, slots.at[place, mine], s2.at[0], r2.at[b, place], home, s)

    @pl.when(jnp.logical_not(at_home))
    def _():
        straight.start()

    @pl.when(at_home)
    def _():
        slots[place, mine, :] = normed[...]

    for source in range(nbatch):
        for j in range(sub):
            @pl.when(jnp.logical_not((source == b) & (b * sub + j == s)))
            def _():
                remote(
                    normed, slots.at[j, pl.ds(source * rows, rows)],
                    s2.at[0], r2.at[source, j], source, b * sub + j,
                ).wait_recv()

    w_copy.wait()
    chunk = 256 if width % 256 == 0 else width
    for c in range(0, width, chunk):
        acc = None
        for j in range(sub):
            term = jnp.dot(
                slots[j], wbuf[j * local : (j + 1) * local, c : c + chunk],
                preferred_element_type=jnp.float32,
            )
            acc = term if acc is None else acc + term
        part[:, c : c + chunk] = acc

    reduces = []
    for k in range(nbatch - 1, 0, -1):
        to = flip(b, k)
        reduces.append(
            remote(
                part.at[pl.ds(pl.multiple_of(to * rows, rows), rows)],
                part_recv.at[k], s3.at[k], r3.at[k], to, s,
            )
        )
        reduces[-1].start()
    for copy in reduces:
        copy.wait_recv()
    owned = part[mine, :]
    for k in range(1, nbatch):
        owned = owned + part_recv[k]
    gath[s] = owned.astype(jnp.bfloat16)

    gathers = []
    for k in range(nseq - 1, 0, -1):
        gathers.append(remote(gath.at[s], gath.at[s], s4.at[k], r4.at[s], b, flip(s, k)))
        gathers[-1].start()
    for source in range(nseq):
        @pl.when(source != s)
        def _():
            remote(gath.at[source], gath.at[source], s4.at[0], r4.at[source], b, source).wait_recv()

        if len(out_ref.shape) == 2:
            out_ref[:, source * width : (source + 1) * width] = gath[source]
        else:
            out_ref[source] = gath[source]

    for copy in copies + sends + reduces + gathers:
        copy.wait_send()

    @pl.when(jnp.logical_not(at_home))
    def _():
        straight.wait_send()


def attend_kernel(
    nseq, length_ref, x_ref, q_ref, fresh_k, fresh_v, keys_hbm, values_hbm, w_hbm, out_ref,
    kext, vext, wbuf, wide_q, stat, o_send, o_recv, st_send, st_recv, heads, attended,
    p_send, p_recv,
    k_sem, v_sem, fk_sem, fv_sem, w_sem, s1, r1, s2, r2, s3, r3,
):
    b = lax.axis_index("batch")
    s = lax.axis_index("seq")
    seqs, shard_len, _ = keys_hbm.shape
    rows, local = x_ref.shape
    here = H // nseq
    pair_rows = 2 * (H // KVH)
    per = 2 * here
    split = pair_rows // per
    depth = shard_len + PAD
    scale = 1.0 / math.sqrt(HD)

    loads = []
    fresh_copies = [
        pltpu.make_async_copy(fresh_k, kext.at[:, pl.ds(shard_len, PAD)], fk_sem),
        pltpu.make_async_copy(fresh_v, vext.at[:, pl.ds(shard_len, PAD)], fv_sem),
    ]
    key_copies = [
        pltpu.make_async_copy(keys_hbm.at[i], kext.at[i, pl.ds(0, shard_len)], k_sem.at[i])
        for i in range(seqs)
    ]
    value_copies = [
        pltpu.make_async_copy(values_hbm.at[i], vext.at[i, pl.ds(0, shard_len)], v_sem.at[i])
        for i in range(seqs)
    ]
    order = list(range(nseq - 1, -1, -1))
    weight_copies = {}
    for k in order:
        to = flip(s, k)
        weight_copies[k] = pltpu.make_async_copy(
            w_hbm.at[:, pl.ds(pl.multiple_of(to * local, local), local)], wbuf.at[k], w_sem.at[k]
        )
    for copy in fresh_copies + key_copies + value_copies + [weight_copies[k] for k in order]:
        copy.start()

    barrier = pltpu.get_barrier_semaphore()
    for k in range(1, nseq):
        signal(barrier, b, flip(s, k))

    wide_q[...] = jnp.zeros_like(wide_q)
    stat[...] = jnp.zeros_like(stat)
    for i in range(seqs):
        for k in range(KVH):
            wide_q[i, k * pair_rows : (k + 1) * pair_rows, k * HD : (k + 1) * HD] = q_ref[
                i, k * pair_rows : (k + 1) * pair_rows
            ]
    for copy in fresh_copies:
        copy.wait()

    columns = KVH * pair_rows
    row = lax.broadcasted_iota(jnp.int32, (depth, columns), 0)
    lane = lax.broadcasted_iota(jnp.int32, (depth, columns), 1)
    step = (lane // here) % 2
    low = s * shard_len
    cached = row < shard_len
    causal = (row >= shard_len) & (row - shard_len <= step)
    for i in range(seqs):
        key_copies[i].wait()
        value_copies[i].wait()
        scores = lax.dot_general(
            kext[i], wide_q[i], (((1,), (1,)), ((), ())), preferred_element_type=jnp.float32
        ) * scale
        length = jnp.full((depth, columns), length_ref[i], jnp.int32)
        fresh_place = length + row - shard_len
        live = (cached & (low + row < length)) | (
            causal & (fresh_place >= low) & (fresh_place < low + shard_len)
        )
        peak = jnp.max(jnp.where(live, scores, lowest), 0, keepdims=True)
        weights = jnp.where(live, jnp.exp(scores - peak), 0.0)
        stat[i : i + 1, :] = peak
        stat[64 + i : 65 + i, :] = jnp.sum(weights, 0, keepdims=True)
        block = lax.dot_general(
            weights.astype(jnp.bfloat16), vext[i], (((0,), (0,)), ((), ())),
            preferred_element_type=jnp.float32,
        )
        for k in range(KVH):
            for g in range(split):
                first = k * pair_rows + g * per
                o_send[k * split + g, i] = block[first : first + per, k * HD : (k + 1) * HD].astype(
                    jnp.bfloat16
                )
    turned = jnp.transpose(stat[...])
    for k in range(nseq):
        st_send[k] = turned[k * per : (k + 1) * per]

    pl.semaphore_wait(barrier, nseq - 1)
    sends = []
    for k in range(nseq - 1, 0, -1):
        to = flip(s, k)
        sends.append(remote(st_send.at[to], st_recv.at[k], s1.at[k], r1.at[k], b, to))
        sends[-1].start()
        sends.append(remote(o_send.at[to], o_recv.at[k], s2.at[k], r2.at[k], b, to))
        sends[-1].start()
    st_recv[0] = st_send[s]
    o_recv[0] = o_send[s]
    for copy in sends:
        copy.wait_recv()

    stats = [st_recv[k] for k in range(nseq)]
    peak = stats[0]
    for k in range(1, nseq):
        peak = jnp.maximum(peak, stats[k])
    factors = [jnp.exp(stats[k] - peak) for k in range(nseq)]
    total = None
    for k in range(nseq):
        term = pltpu.roll(factors[k], 64, 1) * stats[k]
        total = term if total is None else total + term
    for i in range(seqs):
        acc = None
        for k in range(nseq):
            term = factors[k][:, i : i + 1] * o_recv[k, i].astype(jnp.float32)
            acc = term if acc is None else acc + term
        heads[i] = acc / total[:, 64 + i : 65 + i]
    for t in range(2):
        for g in range(here):
            attended[t * seqs : (t + 1) * seqs, g * HD : (g + 1) * HD] = heads[
                :, t * here + g, :
            ].astype(jnp.bfloat16)

    result = x_ref[...].astype(jnp.float32)
    outs = []
    for k in order:
        weight_copies[k].wait()
        value = jnp.dot(attended[...], wbuf[k], preferred_element_type=jnp.float32)
        if k:
            p_send[k] = value.astype(jnp.bfloat16)
            outs.append(remote(p_send.at[k], p_recv.at[k], s3.at[k], r3.at[k], b, flip(s, k)))
            outs[-1].start()
        else:
            own = value
    for copy in outs:
        copy.wait_recv()
    for k in range(1, nseq):
        own = own + p_recv[k].astype(jnp.float32)
    out_ref[...] = (result + own).astype(jnp.bfloat16)
    for copy in sends + outs:
        copy.wait_send()


def rotate(heads, places):
    half = heads.shape[-1] // 2
    freqs = rope_base ** (-(jnp.arange(half).astype(jnp.float32) * 2.0) / heads.shape[-1])
    angles = places[:, None, None] * freqs
    cosine = jnp.cos(angles)
    sine = jnp.sin(angles)
    first = heads[..., :half]
    second = heads[..., half:]
    return jnp.concatenate([first * cosine - second * sine, second * cosine + first * sine], -1)


def shards(tokens, norm_gain, w_qkv, w_out, cache_keys, cache_values, lengths, positions):
    nbatch = lax.axis_size("batch")
    nseq = lax.axis_size("seq")
    seqs = tokens.shape[1]
    local = tokens.shape[2]
    rows = 2 * seqs
    width = w_qkv.shape[1]
    sub = nseq // nbatch
    group = H // KVH
    here = H // nseq
    split = group // here
    query_width = H * HD
    pair_width = KVH * HD
    shard_len = cache_keys.shape[1]
    flat = tokens.reshape(rows, local)
    vmem = pl.BlockSpec(memory_space=pltpu.VMEM)
    hbm = pl.BlockSpec(memory_space=pl.ANY)
    dma = pltpu.SemaphoreType.DMA
    f32 = jnp.float32
    bf16 = jnp.bfloat16

    joined = width % LANES == 0
    projected = pl.pallas_call(
        lambda *refs: project_kernel(nbatch, nseq, *refs),
        name="project",
        out_shape=jax.ShapeDtypeStruct(
            (rows, nseq * width) if joined else (nseq, rows, width), bf16
        ),
        in_specs=[vmem, vmem, hbm],
        out_specs=vmem,
        scratch_shapes=[
            pltpu.VMEM(w_qkv.shape, bf16),
            pltpu.VMEM((8, LANES), f32),
            pltpu.VMEM((nseq, 8, LANES), f32),
            pltpu.VMEM((rows, local), bf16),
            pltpu.VMEM((sub, nbatch * rows, local), bf16),
            pltpu.VMEM((nbatch * rows, width), f32),
            pltpu.VMEM((nbatch, rows, width), f32),
            pltpu.VMEM((nseq, rows, width), bf16),
            dma,
            dma((nseq,)), dma((nseq,)),
            dma((nseq,)), dma((nbatch, sub)),
            dma((nbatch,)), dma((nbatch,)),
            dma((nseq,)), dma((nseq,)),
        ],
        compiler_params=pltpu.CompilerParams(
            collective_id=0, has_side_effects=True, vmem_limit_bytes=40 * 1024 * 1024
        ),
    )(flat, norm_gain.reshape(1, local), w_qkv)
    if not joined:
        projected = jnp.transpose(projected, (1, 0, 2)).reshape(rows, nseq * width)

    places = jnp.concatenate([positions, positions + 1]).astype(f32)
    queries = rotate(
        projected[:, :query_width].astype(f32).reshape(rows, H, HD), places
    ).astype(bf16)
    fresh_keys = rotate(
        projected[:, query_width : query_width + pair_width].astype(f32).reshape(rows, KVH, HD),
        places,
    ).astype(bf16)
    fresh_values = projected[:, query_width + pair_width :]
    queries = jnp.transpose(
        queries.reshape(2, seqs, KVH, split, here, HD), (1, 2, 3, 0, 4, 5)
    ).reshape(seqs, 2 * H, HD)

    def padded(fresh):
        fresh = jnp.transpose(fresh.reshape(2, seqs, pair_width), (1, 0, 2))
        return jnp.pad(fresh, ((0, 0), (0, PAD - 2), (0, 0)))

    depth = shard_len + PAD
    per = 2 * here
    smem = pl.BlockSpec(memory_space=pltpu.SMEM)
    mixed = pl.pallas_call(
        lambda *refs: attend_kernel(nseq, *refs),
        name="attend",
        out_shape=jax.ShapeDtypeStruct((rows, local), bf16),
        in_specs=[smem, vmem, vmem, hbm, hbm, hbm, hbm, hbm],
        out_specs=vmem,
        scratch_shapes=[
            pltpu.VMEM((seqs, depth, pair_width), bf16),
            pltpu.VMEM((seqs, depth, pair_width), bf16),
            pltpu.VMEM((nseq, w_out.shape[0], local), bf16),
            pltpu.VMEM((seqs, 2 * H, pair_width), bf16),
            pltpu.VMEM((LANES, 2 * H), f32),
            pltpu.VMEM((nseq, seqs, per, HD), bf16),
            pltpu.VMEM((nseq, seqs, per, HD), bf16),
            pltpu.VMEM((nseq, per, LANES), f32),
            pltpu.VMEM((nseq, per, LANES), f32),
            pltpu.VMEM((seqs, per, HD), f32),
            pltpu.VMEM((rows, here * HD), bf16),
            pltpu.VMEM((nseq, rows, local), bf16),
            pltpu.VMEM((nseq, rows, local), bf16),
            dma((seqs,)), dma((seqs,)), dma, dma, dma((nseq,)),
            dma((nseq,)), dma((nseq,)),
            dma((nseq,)), dma((nseq,)),
            dma((nseq,)), dma((nseq,)),
        ],
        compiler_params=pltpu.CompilerParams(
            collective_id=1, has_side_effects=True, vmem_limit_bytes=60 * 1024 * 1024
        ),
    )(lengths, flat, queries, padded(fresh_keys), padded(fresh_values), cache_keys, cache_values, w_out)
    return mixed.reshape(2, seqs, local)


def solution(mesh):
    return jax.shard_map(
        shards,
        mesh=mesh,
        in_specs=(
            P(None, "batch", "seq"),
            P("seq"),
            P("batch", "seq"),
            P("seq", None),
            P("batch", "seq", None),
            P("batch", "seq", None),
            P("batch"),
            P("batch"),
        ),
        out_specs=P(None, "batch", "seq"),
        check_vma=False,
    )
```

time: 238 us -> 113 us (0.47)
  the two profiles are of different devices: /device:TPU:0 before, /device:TPU:10 now
where the time goes in v1:
time: 113 us; the launch traced here: 112 us
  Pallas kernels  101 us (89%)
  local copies, waits for them, and re-layouts  8.48 us (8%)
  other arithmetic  2.67 us (2%)
    pallas_call x1, Pallas kernels, shards(): pl.pallas_call(lambda *refs: project_kernel(nbatch, nseq, *refs), name='p...  71.4 us
    pallas_call x1, Pallas kernels, shards(): pl.pallas_call(lambda *refs: attend_kernel(nseq, *refs), name='attend', o...  29.6 us
    unnamed x7, local copies, waits for them, and re-layouts  5.01 us

profile of v1, /device:TPU:10, one launch (start us, length us, event | category | flops | bytes accessed | tf_op | source)
XLA Modules:
  0.0 112.2 jit_solution(9029129215707883549)
XLA Ops:
  0.0 0.7 broadcast_add_fusion
  0.7 0.7 add_convert_fusion.2
  1.4 0.7 reshape.144.refs_1_
  2.1 0.1 multiply_cosine_fusion
  2.2 0.0 copy-start
  2.2 2.5 %copy-done = bf16[2048,1280]{1,0:T(8,128)(2,1)S(1)} copy-done((bf16[2048,1280]{1,0:T(8,128)(2,1)S(1)}, bf16[2048,1280]{1,0:T(8,128)(2,1)}, u32[]{:S(2)}) %copy-start) | copy-done | bytes 5242904
  4.7 0.0 copy-start.1
  4.7 0.8 copy-done.1
  5.6 71.4 %project.1 = bf16[32,10240]{1,0:T(8,128)(2,1)S(1)} custom-call(bf16[32,1024]{1,0:T(8,128)(2,1)S(1)} %bitcast.21, bf16[1,1024]{1,0:T(2,128)(2,1)S(1)} %reshape.144.refs_1_, bf16[2048,1280]{1,0:T(8,128)(2,1)S(1)} %copy-done), custom_call_target="tpu_custom_call" | custom-call | tf_op jit(solution)/shard_map/project/pallas_call | solution.py:355
  77.0 0.1 copy.16
  77.1 0.1 subtract_convert_fusion.1
  77.2 0.1 pad_maximum_fusion
  77.3 0.1 copy.17
  77.4 0.1 convert_bitcast_fusion
  77.5 0.2 copy.12
  77.7 0.5 subtract_convert_fusion
  78.2 0.3 maximum_bitcast_fusion
  78.5 0.9 copy.9
  79.4 0.9 pad.7.refs_3_
  80.3 0.9 pad.8.refs_4_
  81.2 29.6 %attend.1 = bf16[32,1024]{1,0:T(8,128)(2,1)} custom-call(s32[16]{0:T(128)} %refs_0_.1, bf16[32,1024]{1,0:T(8,128)(2,1)} %bitcast.20, bf16[16,128,128]{2,1,0:T(8,128)(2,1)} %bitcast.25, bf16[16,16,1024]{2,1,0:T(8,128)(2,1)} %pad.7.refs_3_, bf16[16,16,1024]{2,1,0:T(8,128)(2,1)} %pad.8.refs_4_, bf16[16,128,1024]{2,1,0:T(8,128)(2,1)} %refs_5_.1, ...), custom_call_target="tpu_custom_call" | custom-call | tf_op jit(solution)/shard_map/attend/pallas_call | solution.py:405
  110.7 1.5 %copy.19 = bf16[2,16,1024]{2,1,0:T(8,128)(2,1)} copy(bf16[2,16,1024]{2,1,0:T(8,128)(2,1)} %bitcast.27) | data formatting | bytes 131072
  (4 shorter events, 0.1 us)
Async XLA Ops:
  2.2 2.5 %copy-start = (bf16[2048,1280]{1,0:T(8,128)(2,1)S(1)}, bf16[2048,1280]{1,0:T(8,128)(2,1)}, u32[]{:S(2)}) copy-start(bf16[2048,1280]{1,0:T(8,128)(2,1)} %refs_2_.1) | copy-start | bytes 15728644
  4.7 0.8 copy-start.1

commit v2 on v1

--- a/solution.py
+++ b/solution.py
@@ -47,8 +47,8 @@
 
 def project_kernel(
     nbatch, nseq, x_ref, gain_ref, w_hbm, out_ref,
-    wbuf, stat_send, stat_recv, normed, slots, part, part_recv, gath,
-    w_sem, s1, r1, s2, r2, s3, r3, s4, r4,
+    wbuf, stat_send, stat_recv, normed, plane, slots, part, part_recv, gath,
+    w_sem, s1, r1, s2, r2, s3, r3, s4, r4, s5, r5, s6, r6, s7,
 ):
     b = lax.axis_index("batch")
     s = lax.axis_index("seq")
@@ -60,17 +60,11 @@
 
     home = s // sub
     place = s % sub
-    at_home = home == b
     barrier = pltpu.get_barrier_semaphore()
     for k in range(1, nseq):
         signal(barrier, b, flip(s, k))
     for k in range(1, nbatch):
         signal(barrier, flip(b, k), s)
-    for source in range(nbatch):
-        for j in range(sub):
-            @pl.when(jnp.logical_not((source == b) & (b * sub + j == s)))
-            def _():
-                signal(barrier, source, b * sub + j)
 
     widened = x_ref[...].astype(jnp.float32)
     sums = jnp.sum(widened * widened, -1, keepdims=True)
@@ -82,7 +76,7 @@
         packed = jnp.where(lane == i, sums[i * 8 : (i + 1) * 8], packed)
     stat_send[...] = packed
 
-    pl.semaphore_wait(barrier, (nseq - 1) + (nbatch - 1) + nseq - jnp.where(at_home, 1, 0))
+    pl.semaphore_wait(barrier, (nseq - 1) + (nbatch - 1))
 
     copies = []
     for k in range(nseq - 1, 0, -1):
@@ -98,31 +92,52 @@
     column = jnp.concatenate([inverse[:, i * span : i * span + 1] for i in range(tiles)], 0)
     normed[...] = (widened * column * gain).astype(jnp.bfloat16)
 
-    mine = pl.ds(pl.multiple_of(b * rows, rows), rows)
+    def strip(batch):
+        return pl.ds(pl.multiple_of(batch * rows, rows), rows)
+
+    mine = strip(b)
     sends = []
-    for k in range(nseq - 1, 0, -1):
-        sends.append(
-            remote(normed, slots.at[place, mine], s2.at[k], r2.at[b, place], home, flip(s, k))
-        )
+    for k in range(nbatch - 1, 0, -1):
+        peer = flip(home, k) * sub + place
+        sends.append(remote(normed, plane.at[k], s2.at[k], r2.at[k], b, peer))
         sends[-1].start()
-    straight = remote(normed, slots.at[place, mine], s2.at[0], r2.at[b, place], home, s)
-
-    @pl.when(jnp.logical_not(at_home))
-    def _():
-        straight.start()
-
-    @pl.when(at_home)
-    def _():
-        slots[place, mine, :] = normed[...]
-
-    for source in range(nbatch):
-        for j in range(sub):
-            @pl.when(jnp.logical_not((source == b) & (b * sub + j == s)))
-            def _():
-                remote(
-                    normed, slots.at[j, pl.ds(source * rows, rows)],
-                    s2.at[0], r2.at[source, j], source, b * sub + j,
-                ).wait_recv()
+    onward = []
+    for k in range(nbatch):
+        target = flip(home, k)
+        held = plane.at[k] if k else normed
+        copy = remote(held, slots.at[place, mine], s5.at[k], r5.at[b], target, s)
+        onward.append((target, copy))
+        if k:
+            remote(normed, plane.at[k], s2.at[k], r2.at[k], b, target * sub + place).wait_recv()
+
+        @pl.when(target != b)
+        def _():
+            copy.start()
+
+        @pl.when(target == b)
+        def _():
+            slots[place, mine, :] = held[...]
+
+    def relay(m, q):
+        block = slots.at[place, strip(flip(b, m))]
+        to = home * sub + flip(place, q)
+        return remote(block, block, s6.at[q, m], r6.at[place, flip(b, m)], b, to)
+
+    for m in range(nbatch):
+        other = flip(b, m)
+        if m:
+            block = slots.at[place, strip(other)]
+            remote(block, block, s5.at[0], r5.at[other], other, s).wait_recv()
+        for q in range(1, sub):
+            sends.append(relay(m, q))
+            sends[-1].start()
+    for q in range(1, sub):
+        for m in range(nbatch):
+            other = flip(place, q)
+            block = slots.at[other, strip(flip(b, m))]
+            remote(
+                block, block, s6.at[q, m], r6.at[other, flip(b, m)], b, home * sub + other
+            ).wait_recv()
 
     w_copy.wait()
     chunk = 256 if width % 256 == 0 else width
@@ -154,11 +169,21 @@
     gath[s] = owned.astype(jnp.bfloat16)
 
     gathers = []
-    for k in range(nseq - 1, 0, -1):
-        gathers.append(remote(gath.at[s], gath.at[s], s4.at[k], r4.at[s], b, flip(s, k)))
+
+    def spread(source, send_sem, to):
+        gathers.append(remote(gath.at[source], gath.at[source], send_sem, r4.at[source], b, to))
         gathers[-1].start()
+
+    for k in range(nbatch - 1, 0, -1):
+        spread(s, s4.at[k], flip(home, k) * sub + place)
+    for k in range(nbatch):
+        source = flip(home, k) * sub + place
+        if k:
+            remote(gath.at[source], gath.at[source], s4.at[k], r4.at[source], b, source).wait_recv()
+        for q in range(1, sub):
+            spread(source, s7.at[q, k], home * sub + flip(place, q))
     for source in range(nseq):
-        @pl.when(source != s)
+        @pl.when(source % sub != place)
         def _():
             remote(gath.at[source], gath.at[source], s4.at[0], r4.at[source], b, source).wait_recv()
 
@@ -169,10 +194,10 @@
 
     for copy in copies + sends + reduces + gathers:
         copy.wait_send()
-
-    @pl.when(jnp.logical_not(at_home))
-    def _():
-        straight.wait_send()
+    for target, copy in onward:
+        @pl.when(target != b)
+        def _():
+            copy.wait_send()
 
 
 def attend_kernel(
@@ -365,18 +390,22 @@
             pltpu.VMEM((8, LANES), f32),
             pltpu.VMEM((nseq, 8, LANES), f32),
             pltpu.VMEM((rows, local), bf16),
+            pltpu.VMEM((nbatch, rows, local), bf16),
             pltpu.VMEM((sub, nbatch * rows, local), bf16),
             pltpu.VMEM((nbatch * rows, width), f32),
             pltpu.VMEM((nbatch, rows, width), f32),
             pltpu.VMEM((nseq, rows, width), bf16),
             dma,
             dma((nseq,)), dma((nseq,)),
-            dma((nseq,)), dma((nbatch, sub)),
             dma((nbatch,)), dma((nbatch,)),
-            dma((nseq,)), dma((nseq,)),
+            dma((nbatch,)), dma((nbatch,)),
+            dma((nbatch,)), dma((nseq,)),
+            dma((nbatch,)), dma((nbatch,)),
+            dma((sub, nbatch)), dma((sub, nbatch)),
+            dma((sub, nbatch)),
         ],
         compiler_params=pltpu.CompilerParams(
-            collective_id=0, has_side_effects=True, vmem_limit_bytes=40 * 1024 * 1024
+            collective_id=0, has_side_effects=True, vmem_limit_bytes=60 * 1024 * 1024
         ),
     )(flat, norm_gain.reshape(1, local), w_qkv)
     if not joined:

time: 113 us -> 94.8 us (0.84)
  the two profiles are of different devices: /device:TPU:10 before, /device:TPU:0 now
where the time goes in v2:
time: 94.8 us; the launch traced here: 94.5 us
  Pallas kernels  84 us (89%)
  local copies, waits for them, and re-layouts  5.75 us (6%)
  other arithmetic  4.58 us (5%)
    pallas_call x1, Pallas kernels, shards(): pl.pallas_call(lambda *refs: project_kernel(nbatch, nseq, *refs), name='p...  51 us
    pallas_call x1, Pallas kernels, shards(): pl.pallas_call(lambda *refs: attend_kernel(nseq, *refs), name='attend', o...  33 us

profile of v2, /device:TPU:0, one launch (start us, length us, event | category | flops | bytes accessed | tf_op | source)
XLA Modules:
  0.0 94.5 jit_solution(7975012050177463419)
XLA Ops:
  0.0 0.7 broadcast_add_fusion
  0.7 0.7 add_convert_fusion.2
  1.4 1.3 %reshape.144.refs_1_ = bf16[1,1024]{1,0:T(2,128)(2,1)} reshape(bf16[1024]{0:T(1024)(128)(2,1)} %param.9) | data formatting | bytes 4096 | tf_op jit(solution)/shard_map/reshape | solution.py:410
  2.7 0.1 multiply_cosine_fusion
  2.8 51.0 %project.1 = bf16[32,10240]{1,0:T(8,128)(2,1)} custom-call(bf16[32,1024]{1,0:T(8,128)(2,1)} %bitcast.25, bf16[1,1024]{1,0:T(2,128)(2,1)} %reshape.144.refs_1_, bf16[2048,1280]{1,0:T(8,128)(2,1)} %refs_2_.1), custom_call_target="tpu_custom_call" | custom-call | tf_op jit(solution)/shard_map/project/pallas_call | solution.py:380
  53.8 0.9 fusion
  54.7 0.1 copy.16
  54.8 0.1 subtract_convert_fusion.1
  55.0 0.1 pad_maximum_fusion
  55.1 0.1 copy.17
  55.2 1.1 %convert_bitcast_fusion = f32[4,8,64,128]{3,1,2,0:T(8,128)S(1)} fusion(bf16[32,10240]{1,0:T(8,128)(2,1)} %project.1), kind=kLoop, calls=%fused_computation | loop fusion | flops 262144 | bytes 1572864
  56.3 0.2 copy.12
  56.5 0.5 subtract_convert_fusion
  57.0 0.3 maximum_bitcast_fusion
  57.3 0.9 copy.9
  58.2 0.8 pad.7.refs_3_
  59.1 0.9 pad.8.refs_4_
  60.0 33.0 %attend.1 = bf16[32,1024]{1,0:T(8,128)(2,1)} custom-call(s32[16]{0:T(128)} %refs_0_.1, bf16[32,1024]{1,0:T(8,128)(2,1)} %bitcast.26, bf16[16,128,128]{2,1,0:T(8,128)(2,1)} %bitcast.23, bf16[16,16,1024]{2,1,0:T(8,128)(2,1)} %pad.7.refs_3_, bf16[16,16,1024]{2,1,0:T(8,128)(2,1)} %pad.8.refs_4_, bf16[16,128,1024]{2,1,0:T(8,128)(2,1)} %refs_5_.1, ...), custom_call_target="tpu_custom_call" | custom-call | tf_op jit(solution)/shard_map/attend/pallas_call | solution.py:434
  93.0 1.5 %copy.19 = bf16[2,16,1024]{2,1,0:T(8,128)(2,1)} copy(bf16[2,16,1024]{2,1,0:T(8,128)(2,1)} %bitcast.27) | data formatting | bytes 131072
  (3 shorter events, 0.1 us)
